TPU v7x, 32 devices: a whole 2x2x4 slice. The times are simulated.
32 devices in a mesh: seq: 8 (over z, y), head: 4 (over x, core).
Axes of the slice: x: 2, y: 2, z: 4, core: 2. Of those that a mesh axis runs over, the one named last changes fastest.
Arguments:
- residual: bfloat16 [4096, 3072], P('seq', 'head'), may hold values from -6 to 6
- q_self: bfloat16 [4096, 3072], P('seq', 'head'), may hold values from -6 to 6
- k_self: bfloat16 [4096, 3072], P('seq', 'head'), may hold values from -6 to 6
- v_self: bfloat16 [4096, 3072], P('seq', 'head'), may hold values from -6 to 6
- w_out: bfloat16 [3072, 3072], P('head'), may hold values from -0.109375 to 0.109375
- norm_gain: float32 [3072], replicated, may hold values from 0.5 to 1.5
- w_query: bfloat16 [3072, 3072], P('seq', 'head')
- w_cache: bfloat16 [3072, 2048], P('seq', 'head')
- block_doc: int32 [8], replicated, may hold values from 0 to 2, never falling along the last dimension, each value on 1 to 4 neighbouring positions
- tail_len: int32 [8], replicated, may hold values from 1 to 512
Outputs:
- hidden: bfloat16 [4096, 3072], P('seq', 'head')
- cross_context: bfloat16 [4096, 3072], P('seq', 'head')
Inputs may be any that keep to these rules, and one draw needn't show every extreme that they name: block_doc never falls along the blocks; each document covers 1 to 4 consecutive blocks, and some document covers exactly 4. `tail_len`: read only for the last block of a document.
All inputs are finite; a program needn't handle non-finite values.
Results may differ from a plain program's by a relative error of at most 0.0078.
Values may be sent and summed in bfloat16 or wider, within the bound.
No kernel may reach another device: no remote copies, remote signals or barrier semaphores. Data moves between devices by JAX's collectives and lax.ppermute only.
A program may use at most 128 MiB of HBM per device.

v0:
```python
import math
import jax
import jax.numpy as jnp
from jax import lax
from jax.sharding import PartitionSpec as P

D = 3072
HEAD_DIM = 128
WINDOW = 2048
DOC_MAX = 2560
WIN_BLOCKS = 4
DOC_BLOCKS = 5
EPSILON = 1e-06


def passed_along(block, axis, distance):
    devices = range(lax.axis_size(axis))
    route = [(i - distance, i) for i in devices if i - distance in devices]
    return lax.ppermute(block, axis, route)


def block_valid(block_doc, tail_len, tok_rows):
    following = jnp.concatenate([block_doc[1:], jnp.full((1,), -1, jnp.int32)])
    closing = following != block_doc
    within = jnp.arange(tok_rows, dtype=jnp.int32)
    return jnp.logical_or(jnp.logical_not(closing)[:, None], within[None, :] < tail_len[:, None])


def permitted(query_block, key_blocks, block_doc, valid_tokens, tok_rows, reach_tokens):
    inside = key_blocks >= 0
    safe_blocks = jnp.maximum(key_blocks, 0)
    own_doc = jnp.take(block_doc, query_block)
    same_doc = jnp.logical_and(inside, jnp.take(block_doc, safe_blocks) == own_doc)
    live_keys = jnp.logical_and(same_doc[:, None], jnp.take(valid_tokens, safe_blocks, axis=0))
    within = jnp.arange(tok_rows, dtype=jnp.int32)
    query_pos = query_block * tok_rows + within
    key_pos = (key_blocks[:, None] * tok_rows + within[None, :]).reshape(-1)
    distance = query_pos[:, None] - key_pos[None, :]
    near = jnp.logical_and(distance >= 0, distance < reach_tokens)
    return jnp.logical_and(near, live_keys.reshape(-1)[None, :])


def attend(queries, keys, values, allowed):
    row_count, head_count, head_dim = queries.shape
    group_size = head_count // keys.shape[1]
    scaling = 1.0 / math.sqrt(head_dim)

    def one_head(head_index):
        query_head = lax.dynamic_index_in_dim(queries, head_index, 1, keepdims=False)
        key_head = lax.dynamic_index_in_dim(keys, head_index // group_size, 1, keepdims=False)
        value_head = lax.dynamic_index_in_dim(values, head_index // group_size, 1, keepdims=False)
        scores = (
            lax.dot_general(
                query_head, key_head, (((1,), (1,)), ((), ())), preferred_element_type=jnp.float32
            )
            * scaling
        )
        scores = jnp.where(allowed, scores, -1e30)
        row_peak = jnp.max(scores, axis=1, keepdims=True)
        weights = jnp.exp(scores - row_peak)
        row_total = jnp.sum(weights, axis=1, keepdims=True)
        blended = jnp.dot(
            weights.astype(jnp.bfloat16), value_head, preferred_element_type=jnp.float32
        )
        return (blended / row_total).astype(jnp.bfloat16)

    per_head = lax.map(one_head, jnp.arange(head_count, dtype=jnp.int32))
    return jnp.transpose(per_head, (1, 0, 2)).reshape(row_count, head_count * head_dim)


def local(
    residual, q_self, k_self, v_self, w_out, norm_gain, w_query, w_cache, block_doc, tail_len
):
    tok_rows = residual.shape[0]
    local_heads = q_self.shape[1] // HEAD_DIM
    local_kv = w_cache.shape[1] // (2 * HEAD_DIM)
    query_width = local_heads * HEAD_DIM
    block_index = lax.axis_index("seq")
    valid_tokens = block_valid(block_doc, tail_len, tok_rows)
    stacked = jnp.concatenate([k_self, v_self], axis=1)
    earlier = []
    for offset in range(WIN_BLOCKS, 0, -1):
        earlier.append(passed_along(stacked, "seq", offset))
    window = jnp.concatenate(earlier + [stacked], axis=0)
    key_blocks = block_index - WIN_BLOCKS + jnp.arange(WIN_BLOCKS + 1, dtype=jnp.int32)
    allowed = permitted(block_index, key_blocks, block_doc, valid_tokens, tok_rows, WINDOW)
    context = attend(
        q_self.reshape(tok_rows, local_heads, HEAD_DIM),
        window[:, :query_width].reshape(-1, local_heads, HEAD_DIM),
        window[:, query_width:].reshape(-1, local_heads, HEAD_DIM),
        allowed,
    )
    partial_terms = jnp.dot(context, w_out, preferred_element_type=jnp.float32)
    own_columns = residual.shape[1]
    column_share = lax.psum_scatter(partial_terms, "head", scatter_dimension=1, tiled=True)
    hidden = (residual.astype(jnp.float32) + column_share).astype(jnp.bfloat16)
    wide = hidden.astype(jnp.float32)
    square_total = lax.psum(jnp.sum(wide * wide, axis=1), "head")
    inverse_rms = lax.rsqrt(square_total / D + EPSILON)
    gain_share = lax.dynamic_slice_in_dim(
        norm_gain, lax.axis_index("head") * own_columns, own_columns, 0
    )
    normed_share = (wide * inverse_rms[:, None] * gain_share).astype(jnp.bfloat16)
    normed = lax.all_gather(normed_share, "head", axis=1, tiled=True)
    query_sum = jnp.dot(
        normed,
        lax.all_gather(w_query, "seq", axis=0, tiled=True),
        preferred_element_type=jnp.float32,
    )
    cache_sum = jnp.dot(
        normed,
        lax.all_gather(w_cache, "seq", axis=0, tiled=True),
        preferred_element_type=jnp.float32,
    )
    cross_queries = query_sum.astype(jnp.bfloat16)
    cache_rows = cache_sum.astype(jnp.bfloat16)
    earlier_cache = []
    for offset in range(DOC_BLOCKS - 1, 0, -1):
        earlier_cache.append(passed_along(cache_rows, "seq", offset))
    history = jnp.concatenate(earlier_cache + [cache_rows], axis=0)
    doc_key_blocks = block_index - DOC_BLOCKS + 1 + jnp.arange(DOC_BLOCKS, dtype=jnp.int32)
    doc_allowed = permitted(block_index, doc_key_blocks, block_doc, valid_tokens, tok_rows, DOC_MAX)
    kv_width = local_kv * HEAD_DIM
    cross_context = attend(
        cross_queries.reshape(tok_rows, local_heads, HEAD_DIM),
        history[:, :kv_width].reshape(-1, local_kv, HEAD_DIM),
        history[:, kv_width:].reshape(-1, local_kv, HEAD_DIM),
        doc_allowed,
    )
    return (hidden, cross_context)


def solution(mesh):
    in_specs = (
        P("seq", "head"),
        P("seq", "head"),
        P("seq", "head"),
        P("seq", "head"),
        P("head", None),
        P(),
        P("seq", "head"),
        P("seq", "head"),
        P(),
        P(),
    )
    out_specs = (P("seq", "head"), P("seq", "head"))
    return jax.shard_map(local, mesh=mesh, in_specs=in_specs, out_specs=out_specs, check_vma=False)
```

profile of v0, /device:TPU:17, one launch (start us, length us, event | category | flops | bytes accessed | tf_op | source)
XLA Modules:
  0.0 584.7 jit_solution(10366672590483666135)
XLA Ops:
  12.3 4.2 collective-permute-start.1
  23.3 2.3 copy.13
  25.6 23.7 %collective-permute-done = bf16[512,1536]{0,1:T(8,128)(2,1)} collective-permute-done((bf16[512,1536]{0,1:T(8,128)(2,1)S(1)}, bf16[512,1536]{0,1:T(8,128)(2,1)}, u32[]{:S(2)}, u32[]{:S(2)}) %collective-permute-start) | collective-permute-done | bytes 1572896 | tf_op jit(solution)/shard_map/ppermute | solution.py:19
  50.7 33.1 %collective-permute-done.1 = bf16[512,1536]{0,1:T(8,128)(2,1)} collective-permute-done((bf16[512,1536]{0,1:T(8,128)(2,1)S(1)}, bf16[512,1536]{0,1:T(8,128)(2,1)}, u32[]{:S(2)}, u32[]{:S(2)}) %collective-permute-start.1) | collective-permute-done | bytes 1572896 | tf_op jit(solution)/shard_map/ppermute | solution.py:19
  85.4 66.0 %collective-permute-done.2 = bf16[512,1536]{0,1:T(8,128)(2,1)} collective-permute-done((bf16[512,1536]{0,1:T(8,128)(2,1)S(1)}, bf16[512,1536]{0,1:T(8,128)(2,1)}, u32[]{:S(2)}, u32[]{:S(2)}) %collective-permute-start.2) | collective-permute-done | bytes 1572896 | tf_op jit(solution)/shard_map/ppermute | solution.py:19
  152.9 66.9 %collective-permute-done.3 = bf16[512,1536]{0,1:T(8,128)(2,1)} collective-permute-done((bf16[512,1536]{0,1:T(8,128)(2,1)S(1)}, bf16[512,1536]{0,1:T(8,128)(2,1)}, u32[]{:S(2)}, u32[]{:S(2)}) %collective-permute-start.3) | collective-permute-done | bytes 1572896 | tf_op jit(solution)/shard_map/ppermute | solution.py:19
  221.4 3.4 fusion.60
  224.8 53.3 %while.27 = (s32[]{:T(128)}, bf16[6,512,128]{1,2,0:T(8,128)(2,1)S(1)}, s32[6]{0:T(128)S(1)}, bf16[512,6,128]{0,2,1:T(8,128)(2,1)}, bf16[2560,6,128]{0,2,1:T(8,12...) while((s32[]{:T(128)}, ...), condition=%wide.region_3.6_spmd.clone, body=%wide.region_0.5_spmd.clone.sunk | while | flops 686947328 | bytes 17852076 | solution.py:67
  227.5 3.2 fusion.80
  231.6 2.0 fusion.82
  236.4 3.2 fusion.80
  245.3 3.2 fusion.80
  254.1 3.2 fusion.80
  263.0 3.2 fusion.80
  271.9 3.2 fusion.80
  278.1 6.9 %fusion.61 = f32[512,3072]{1,0:T(8,128)} fusion(bf16[512,768]{0,1:T(8,128)(2,1)S(1)} %bitcast.88, bf16[768,3072]{1,0:T(8,128)(2,1)} %param.22), kind=kOutput, calls=%fused_computation.87 | convolution fusion | flops 2415919104 | bytes 11796480 | tf_op jit(solution)/shard_map/dot_general | solution.py:93
  286.4 55.4 %reduce-scatter.2.cloned.1.call-done = f32[512,768]{1,0:T(8,128)} async-done(((f32[512,3072]{1,0:T(8,128)}), f32[512,768]{1,0:T(8,128)}) %reduce-scatter.2.cloned.1.call-update) | async-done | bytes 1572880 | tf_op jit(solution)/shard_map/reduce_scatter | solution.py:95
  343.5 5.9 %psum.7 = f32[512]{0:T(512)S(1)} all-reduce(f32[512]{0:T(512)S(1)} %get-tuple-element.300), channel_id=1, replica_groups=mesh['seq'=8,'head'=4] {'head'}, use_global_device_ids=true, to_apply=%region_6.9 | all-reduce | flops 512 | bytes 4096 | tf_op jit(solution)/shard_map/psum | solution.py:98
  351.2 29.0 %all-gather.4.cloned.1.call-done = bf16[512,3072]{1,0:T(8,128)(2,1)} async-done(((bf16[512,768]{1,0:T(8,128)(2,1)}), bf16[512,3072]{1,0:T(8,128)(2,1)}) %all-gather.4.cloned.1.call-update) | async-done | bytes 3145744 | tf_op jit(solution)/shard_map/all_gather | solution.py:104
  380.1 4.6 convolution_convert_fusion.1
  386.1 4.0 collective-permute-start.5
  392.0 2.1 collective-permute-start.7
  394.1 102.8 %all-gather.6.cloned.1.call-done = bf16[3072,768]{1,0:T(8,128)(2,1)} async-done(((bf16[384,768]{1,0:T(8,128)(2,1)}), bf16[3072,768]{1,0:T(8,128)(2,1)}) %all-gather.6.cloned.1.call-update) | async-done | bytes 4718608 | tf_op jit(solution)/shard_map/all_gather | solution.py:107
  496.9 5.9 %convolution_convert_fusion = bf16[512,768]{1,0:T(8,128)(2,1)S(1)} fusion(bf16[512,3072]{1,0:T(8,128)(2,1)} %all-gather.4.cloned.1.call-done, bf16[3072,768]{1,0:T(8,128)(2,1)} %all-gather.6.cloned.1.call-done), kind=kOutput, calls=%fused_computation.55 | convolution fusion | flops 2416312320 | bytes 8650752 | tf_op jit(solution)/shard_map/dot_general | solution.py:105
  505.3 10.2 %collective-permute-done.7 = bf16[512,512]{1,0:T(8,128)(2,1)S(1)} collective-permute-done((bf16[512,512]{1,0:T(8,128)(2,1)S(1)}, bf16[512,512]{1,0:T(8,128)(2,1)S(1)}, u32[]{:S(2)}, u32[]{:S(2)}) %collective-permute-start.7) | collective-permute-done | bytes 524320 | tf_op jit(solution)/shard_map/ppermute | solution.py:19
  517.4 58.5 %while.28 = (s32[]{:T(128)}, bf16[6,512,128]{1,2,0:T(8,128)(2,1)S(1)}, s32[6]{0:T(128)S(1)}, bf16[512,6,128]{0,2,1:T(8,128)(2,1)S(1)}, bf16[2560,2,128]{2,0,1:T(...) while((s32[]{:T(128)}, ...), condition=%wide.region_10.13_spmd.clone, body=%wide.region_7.12_spmd.clone.sunk | while | flops 686947328 | bytes 17853756 | solution.py:67
  521.9 3.3 fusion.85
  531.7 3.3 fusion.85
  541.4 3.3 fusion.85
  551.2 3.3 fusion.85
  560.9 3.3 fusion.85
  570.7 3.3 fusion.85
  (125 shorter events, 64.7 us)
Async XLA Ops:
  8.0 333.8 %reduce-scatter.2.cloned.1.call-start = ((), (), s32[]{:S(2)}) async-start(), calls=%async_computation.1 | async-start | bytes 7864320 | tf_op jit(solution)/shard_map/reduce_scatter | solution.py:95
  8.0 12.3 %copy-start = (s32[8]{0:T(128)S(1)}, s32[8]{0:T(128)}, u32[]{:S(2)}) copy-start(s32[8]{0:T(128)} %param.26) | copy-start | bytes 100
  8.1 14.4 %copy-start.3 = (s32[8]{0:T(128)S(1)}, s32[8]{0:T(128)}, u32[]{:S(2)}) copy-start(s32[8]{0:T(128)} %param.27) | copy-start | bytes 100
  11.0 38.2 %collective-permute-start = (bf16[512,1536]{0,1:T(8,128)(2,1)S(1)}, bf16[512,1536]{0,1:T(8,128)(2,1)}, u32[]{:S(2)}, u32[]{:S(2)}) collective-permute-start(bf16[512,1536]{0,1:T(8,128)(2,1)S(1)} %pad_maximum_fusion), channel_id=1, source_target_pairs={{0,16},{4,20},{8,24},{12,28},{1,17},{5,21},{9,25},{13,29},{2,18},{... | collective-permute-start | bytes 4718600 | tf_op jit(solution)/shard_map/ppermute | solution.py:19
  12.3 71.6 %collective-permute-start.1 = (bf16[512,1536]{0,1:T(8,128)(2,1)S(1)}, bf16[512,1536]{0,1:T(8,128)(2,1)}, u32[]{:S(2)}, u32[]{:S(2)}) collective-permute-start(bf16[512,1536]{0,1:T(8,128)(2,1)S(1)} %pad_maximum_fusion), channel_id=1, source_target_pairs={{0,12},{4,16},{8,20},{12,24},{16,28},{1,13},{5,17},{9,21},{13,25},... | collective-permute-start | bytes 4718600 | tf_op jit(solution)/shard_map/ppermute | solution.py:19
  16.5 134.9 %collective-permute-start.2 = (bf16[512,1536]{0,1:T(8,128)(2,1)S(1)}, bf16[512,1536]{0,1:T(8,128)(2,1)}, u32[]{:S(2)}, u32[]{:S(2)}) collective-permute-start(bf16[512,1536]{0,1:T(8,128)(2,1)S(1)} %pad_maximum_fusion), channel_id=1, source_target_pairs={{0,8},{4,12},{8,16},{12,20},{16,24},{20,28},{1,9},{5,13},{9,17},{1... | collective-permute-start | bytes 4718600 | tf_op jit(solution)/shard_map/ppermute | solution.py:19
  18.4 201.3 %collective-permute-start.3 = (bf16[512,1536]{0,1:T(8,128)(2,1)S(1)}, bf16[512,1536]{0,1:T(8,128)(2,1)}, u32[]{:S(2)}, u32[]{:S(2)}) collective-permute-start(bf16[512,1536]{0,1:T(8,128)(2,1)S(1)} %pad_maximum_fusion), channel_id=1, source_target_pairs={{0,4},{4,8},{8,12},{12,16},{16,20},{20,24},{24,28},{1,5},{5,9},{9,... | collective-permute-start | bytes 4718600 | tf_op jit(solution)/shard_map/ppermute | solution.py:19
  285.0 56.8 %copy-start.2 = (bf16[512,768]{1,0:T(8,128)(2,1)S(1)}, bf16[512,768]{1,0:T(8,128)(2,1)}, u32[]{:S(2)}) copy-start(bf16[512,768]{1,0:T(8,128)(2,1)} %param.18) | copy-start | bytes 2359300
  285.0 66.1 %all-gather.8.cloned.1.call-start = ((), (), s32[]{:S(2)}) async-start(), calls=%async_computation.4 | async-start | bytes 3538944 | tf_op jit(solution)/shard_map/all_gather | solution.py:112
  285.6 94.5 %all-gather.4.cloned.1.call-start = ((), (), s32[]{:S(2)}) async-start(), calls=%async_computation.2 | async-start | bytes 3932160 | tf_op jit(solution)/shard_map/all_gather | solution.py:104
  343.5 41.3 %copy-start.1 = (bf16[512,768]{1,0:T(8,128)(2,1)}, bf16[512,768]{1,0:T(8,128)(2,1)S(1)}, u32[]{:S(2)}) copy-start(bf16[512,768]{1,0:T(8,128)(2,1)S(1)} %get-tuple-element.301) | copy-start | bytes 2359300
  350.6 146.4 %all-gather.6.cloned.1.call-start = ((), (), s32[]{:S(2)}) async-start(), calls=%async_computation.3 | async-start | bytes 5308416 | tf_op jit(solution)/shard_map/all_gather | solution.py:107
  384.8 118.3 %collective-permute-start.4 = (bf16[512,512]{1,0:T(8,128)(2,1)S(1)}, bf16[512,512]{1,0:T(8,128)(2,1)}, u32[]{:S(2)}, u32[]{:S(2)}) collective-permute-start(bf16[512,512]{1,0:T(8,128)(2,1)S(1)} %convolution_convert_fusion.1), channel_id=1, source_target_pairs={{0,16},{4,20},{8,24},{12,28},{1,17},{5,21},{9,25},{13,29},{2,18},{... | collective-permute-start | bytes 1572872 | tf_op jit(solution)/shard_map/ppermute | solution.py:19
  386.1 118.1 %collective-permute-start.5 = (bf16[512,512]{1,0:T(8,128)(2,1)S(1)}, bf16[512,512]{1,0:T(8,128)(2,1)}, u32[]{:S(2)}, u32[]{:S(2)}) collective-permute-start(bf16[512,512]{1,0:T(8,128)(2,1)S(1)} %convolution_convert_fusion.1), channel_id=1, source_target_pairs={{0,12},{4,16},{8,20},{12,24},{16,28},{1,13},{5,17},{9,21},{13,25},... | collective-permute-start | bytes 1572872 | tf_op jit(solution)/shard_map/ppermute | solution.py:19
  390.1 115.2 %collective-permute-start.6 = (bf16[512,512]{1,0:T(8,128)(2,1)S(1)}, bf16[512,512]{1,0:T(8,128)(2,1)S(1)}, u32[]{:S(2)}, u32[]{:S(2)}) collective-permute-start(bf16[512,512]{1,0:T(8,128)(2,1)S(1)} %convolution_convert_fusion.1), channel_id=1, source_target_pairs={{0,8},{4,12},{8,16},{12,20},{16,24},{20,28},{1,9},{5,13},{9,17},{1... | collective-permute-start | bytes 1572872 | tf_op jit(solution)/shard_map/ppermute | solution.py:19
  392.0 123.5 %collective-permute-start.7 = (bf16[512,512]{1,0:T(8,128)(2,1)S(1)}, bf16[512,512]{1,0:T(8,128)(2,1)S(1)}, u32[]{:S(2)}, u32[]{:S(2)}) collective-permute-start(bf16[512,512]{1,0:T(8,128)(2,1)S(1)} %convolution_convert_fusion.1), channel_id=1, source_target_pairs={{0,4},{4,8},{8,12},{12,16},{16,20},{20,24},{24,28},{1,5},{5,9},{9,... | collective-permute-start | bytes 1572872 | tf_op jit(solution)/shard_map/ppermute | solution.py:19
Sparse Core Ops, SparseCore 0:
  285.1 56.6 reduce-scatter.1
Sparse Core Ops, SparseCore 1:
  287.7 57.5 all-gather.7
  350.6 29.4 all-gather.3
  382.2 114.7 all-gather.5
where the time goes:
time: 587 us; the launch traced here: 585 us
  waiting for transfers between devices  388 us (66%)
  matrix products  74.1 us (13%)
  loops' own time  35.9 us (6%)
  local copies, waits for them, and re-layouts  31.7 us (5%)
  starting transfers between devices  18.8 us (3%)
  between operations  16.6 us (3%)
  other arithmetic  13.5 us (2%)
  blocking collectives  5.87 us (1%)
    ppermute x8, waiting for transfers between devices, passed_along(): return lax.ppermute(block, axis, route)  200 us
    all_gather x1, waiting for transfers between devices, local(): lax.all_gather(w_query, 'seq', axis=0, tiled=True)  103 us
    reduce_scatter x1, waiting for transfers between devices, local(): lax.psum_scatter(partial_terms, 'head', scatter_dimension=1, tiled=True)  55.4 us
    dot_general x12, matrix products, one_head(): lax.dot_general(query_head, key_head, (((1,), (1,)), ((), ())), preferred...  39.3 us
    another operation x2, loops' own time, attend(): per_head = lax.map(one_head, jnp.arange(head_count, dtype=jnp.int32))  35.9 us
    all_gather x1, waiting for transfers between devices, local(): normed = lax.all_gather(normed_share, 'head', axis=1, tiled=True)  29 us
    ppermute x8, starting transfers between devices, passed_along(): return lax.ppermute(block, axis, route)  18.6 us
    dot_general x12, matrix products, one_head(): jnp.dot(weights.astype(jnp.bfloat16), value_head, preferred_element_type=...  17.4 us
  transfers between devices with their start and end apart: 12, of which 8 were waited for; matrix products, arithmetic and copies ran while one was open for 4% of the time, Pallas kernels for 0%

commit v1 on v0

--- a/solution.py
+++ b/solution.py
@@ -11,6 +11,28 @@
 WIN_BLOCKS = 4
 DOC_BLOCKS = 5
 EPSILON = 1e-06
+
+
+def in_order(tiles, dim):
+    tiles = jnp.moveaxis(tiles, 0, dim)
+    shape = tiles.shape
+    return tiles.reshape(*shape[:dim], shape[dim] * shape[dim + 1], *shape[dim + 2 :])
+
+
+def doubled(value, axis):
+    length = lax.axis_size(axis)
+    blocks = value[None]
+    for level in range(length.bit_length() - 1):
+        bit = 1 << level
+        theirs = lax.ppermute(blocks, axis, [(i, i ^ bit) for i in range(length)])
+        both = jnp.stack([blocks, theirs])
+        upper = lax.axis_index(axis) >> level & 1
+        blocks = jnp.where(upper == 0, both, both[::-1]).reshape(-1, *value.shape)
+    return blocks
+
+
+def collect(x, axis, dim):
+    return in_order(doubled(x, axis), dim)
 
 
 def passed_along(block, axis, distance):
@@ -102,11 +124,7 @@
     )
     normed_share = (wide * inverse_rms[:, None] * gain_share).astype(jnp.bfloat16)
     normed = lax.all_gather(normed_share, "head", axis=1, tiled=True)
-    query_sum = jnp.dot(
-        normed,
-        lax.all_gather(w_query, "seq", axis=0, tiled=True),
-        preferred_element_type=jnp.float32,
-    )
+    query_sum = jnp.dot(normed, collect(w_query, "seq", 0), preferred_element_type=jnp.float32)
     cache_sum = jnp.dot(
         normed,
         lax.all_gather(w_cache, "seq", axis=0, tiled=True),

time: 587 us -> 616 us (1.049)
  waiting for transfers between devices: 388 us -> 409 us
  other arithmetic: 13.5 us -> 21.2 us
    ppermute x0 -> x3, waiting for transfers between devices: none -> 125 us  [doubled(): theirs = lax.ppermute(blocks, axis, [(i, i ^ bit) for i in range(length)])]
    all_gather x1 -> x0, waiting for transfers between devices: 103 us -> none  [local(): lax.all_gather(w_query, 'seq', axis=0, tiled=True)]
    ppermute x8, waiting for transfers between devices: 200 us -> 245 us  [passed_along(): return lax.ppermute(block, axis, route)]
    all_gather x1, waiting for transfers between devices: 29 us -> 0.01 us  [local(): normed = lax.all_gather(normed_share, 'head', axis=1, tiled=True)]
    reduce_scatter x1, waiting for transfers between devices: 55.4 us -> 38 us  [local(): lax.psum_scatter(partial_terms, 'head', scatter_dimension=1, tiled=True)]
    unnamed x21 -> x25, local copies, waits for them, and re-layouts: 15 us -> 15.4 us
  transfers between devices with their start and end apart: 12 -> 14, of which waited for: 8 -> 11; matrix products, arithmetic and copies ran while one was open for 4% -> 4% of each run, Pallas kernels for 0% -> 0%
where the time goes in v1:
time: 616 us; the launch traced here: 614 us
  waiting for transfers between devices  409 us (66%)
  matrix products  71.1 us (12%)
  loops' own time  35.3 us (6%)
  local copies, waits for them, and re-layouts  31.9 us (5%)
  starting transfers between devices  23.1 us (4%)
  other arithmetic  21.2 us (3%)
  between operations  16.5 us (3%)
    ppermute x8, waiting for transfers between devices, passed_along(): return lax.ppermute(block, axis, route)  245 us
    ppermute x3, waiting for transfers between devices, doubled(): theirs = lax.ppermute(blocks, axis, [(i, i ^ bit) for i in range(length)])  125 us
    dot_general x12, matrix products, one_head(): lax.dot_general(query_head, key_head, (((1,), (1,)), ((), ())), preferred...  39.4 us
    reduce_scatter x1, waiting for transfers between devices, local(): lax.psum_scatter(partial_terms, 'head', scatter_dimension=1, tiled=True)  38 us
    another operation x2, loops' own time, attend(): per_head = lax.map(one_head, jnp.arange(head_count, dtype=jnp.int32))  35.3 us
    ppermute x8, starting transfers between devices, passed_along(): return lax.ppermute(block, axis, route)  22.9 us
    dot_general x12, matrix products, one_head(): jnp.dot(weights.astype(jnp.bfloat16), value_head, preferred_element_type=...  17.4 us
    unnamed x25, local copies, waits for them, and re-layouts  15.4 us
  transfers between devices with their start and end apart: 14, of which 11 were waited for; matrix products, arithmetic and copies ran while one was open for 4% of the time, Pallas kernels for 0%

profile of v1, /device:TPU:17, one launch (start us, length us, event | category | flops | bytes accessed | tf_op | source)
XLA Modules:
  0.0 613.9 jit_solution(6557726302203959275)
XLA Ops:
  12.3 4.2 collective-permute-start.1
  25.6 23.7 %collective-permute-done = bf16[512,1536]{0,1:T(8,128)(2,1)} collective-permute-done((bf16[512,1536]{0,1:T(8,128)(2,1)S(1)}, bf16[512,1536]{0,1:T(8,128)(2,1)}, u32[]{:S(2)}, u32[]{:S(2)}) %collective-permute-start) | collective-permute-done | bytes 1572896 | tf_op jit(solution)/shard_map/ppermute | solution.py:41
  50.7 33.1 %collective-permute-done.1 = bf16[512,1536]{0,1:T(8,128)(2,1)} collective-permute-done((bf16[512,1536]{0,1:T(8,128)(2,1)S(1)}, bf16[512,1536]{0,1:T(8,128)(2,1)}, u32[]{:S(2)}, u32[]{:S(2)}) %collective-permute-start.1) | collective-permute-done | bytes 1572896 | tf_op jit(solution)/shard_map/ppermute | solution.py:41
  85.4 66.0 %collective-permute-done.2 = bf16[512,1536]{0,1:T(8,128)(2,1)} collective-permute-done((bf16[512,1536]{0,1:T(8,128)(2,1)S(1)}, bf16[512,1536]{0,1:T(8,128)(2,1)}, u32[]{:S(2)}, u32[]{:S(2)}) %collective-permute-start.2) | collective-permute-done | bytes 1572896 | tf_op jit(solution)/shard_map/ppermute | solution.py:41
  152.9 66.9 %collective-permute-done.3 = bf16[512,1536]{0,1:T(8,128)(2,1)} collective-permute-done((bf16[512,1536]{0,1:T(8,128)(2,1)S(1)}, bf16[512,1536]{0,1:T(8,128)(2,1)}, u32[]{:S(2)}, u32[]{:S(2)}) %collective-permute-start.3) | collective-permute-done | bytes 1572896 | tf_op jit(solution)/shard_map/ppermute | solution.py:41
  221.4 3.4 fusion.62
  224.8 52.4 %while.27 = (s32[]{:T(128)}, bf16[6,512,128]{1,2,0:T(8,128)(2,1)S(1)}, s32[6]{0:T(128)S(1)}, bf16[512,6,128]{0,2,1:T(8,128)(2,1)}, bf16[2560,6,128]{0,2,1:T(8,12...) while((s32[]{:T(128)}, ...), condition=%wide.region_3.6_spmd.clone, body=%wide.region_0.5_spmd.clone.sunk | while | flops 686947328 | bytes 17852076 | solution.py:89
  227.3 3.2 fusion.82
  236.1 3.2 fusion.82
  244.8 3.2 fusion.82
  253.6 3.2 fusion.82
  262.3 3.2 fusion.82
  271.0 3.2 fusion.82
  277.3 6.9 %fusion.63 = f32[512,3072]{1,0:T(8,128)} fusion(bf16[512,768]{0,1:T(8,128)(2,1)S(1)} %bitcast.103, bf16[768,3072]{1,0:T(8,128)(2,1)} %param.22), kind=kOutput, calls=%fused_computation.95 | convolution fusion | flops 2415919104 | bytes 11796480 | tf_op jit(solution)/shard_map/dot_general | solution.py:115
  286.0 16.6 %collective-permute-done.4 = bf16[1,384,768]{2,1,0:T(8,128)(2,1)S(1)} collective-permute-done((bf16[1,384,768]{2,1,0:T(8,128)(2,1)S(1)}, bf16[1,384,768]{2,1,0:T(8,128)(2,1)S(1)}, u32[]{:S(2)}, u32[]{:S(2)}) %collective-permute-start.4) | collective-permute-done | bytes 589856 | tf_op jit(solution)/shard_map/ppermute | solution.py:27
  303.0 38.0 %reduce-scatter.2.cloned.1.call-done = f32[512,768]{1,0:T(8,128)} async-done(((f32[512,3072]{1,0:T(8,128)}), f32[512,768]{1,0:T(8,128)}) %reduce-scatter.2.cloned.1.call-update) | async-done | bytes 1572880 | tf_op jit(solution)/shard_map/reduce_scatter | solution.py:117
  342.9 6.0 psum.7
  350.1 9.4 %collective-permute-done.5 = bf16[2,384,768]{2,1,0:T(8,128)(2,1)} collective-permute-done((bf16[2,384,768]{2,1,0:T(8,128)(2,1)S(1)}, bf16[2,384,768]{2,1,0:T(8,128)(2,1)}, u32[]{:S(2)}, u32[]{:S(2)}) %collective-permute-start.5) | collective-permute-done | bytes 1179680 | tf_op jit(solution)/shard_map/ppermute | solution.py:27
  361.5 99.5 %collective-permute-done.6 = bf16[4,384,768]{2,1,0:T(8,128)(2,1)} collective-permute-done((bf16[4,384,768]{2,1,0:T(8,128)(2,1)S(1)}, bf16[4,384,768]{2,1,0:T(8,128)(2,1)}, u32[]{:S(2)}, u32[]{:S(2)}) %collective-permute-start.6) | collective-permute-done | bytes 2359328 | tf_op jit(solution)/shard_map/ppermute | solution.py:27
  463.1 3.0 reverse_select_fusion
  466.1 4.8 convolution_convert_fusion.1
  472.2 8.4 %collective-permute-start.8 = (bf16[512,512]{1,0:T(8,128)(2,1)S(1)}, bf16[512,512]{1,0:T(8,128)(2,1)}, u32[]{:S(2)}, u32[]{:S(2)}) collective-permute-start(bf16[512,512]{1,0:T(8,128)(2,1)S(1)} %convolution_convert_fusion.1), channel_id=1, source_target_pairs={{0,12},{4,16},{8,20},{12,24},{16,28},{1,13},{5,17},{9,21},{13,25},... | collective-permute-start | bytes 1572872 | tf_op jit(solution)/shard_map/ppermute | solution.py:41
  488.5 14.2 %collective-permute-done.8 = bf16[512,512]{1,0:T(8,128)(2,1)} collective-permute-done((bf16[512,512]{1,0:T(8,128)(2,1)S(1)}, bf16[512,512]{1,0:T(8,128)(2,1)}, u32[]{:S(2)}, u32[]{:S(2)}) %collective-permute-start.8) | collective-permute-done | bytes 524320 | tf_op jit(solution)/shard_map/ppermute | solution.py:41
  503.8 17.7 %collective-permute-done.9 = bf16[512,512]{1,0:T(8,128)(2,1)S(1)} collective-permute-done((bf16[512,512]{1,0:T(8,128)(2,1)S(1)}, bf16[512,512]{1,0:T(8,128)(2,1)S(1)}, u32[]{:S(2)}, u32[]{:S(2)}) %collective-permute-start.9) | collective-permute-done | bytes 524320 | tf_op jit(solution)/shard_map/ppermute | solution.py:41
  521.6 23.3 %collective-permute-done.10 = bf16[512,512]{1,0:T(8,128)(2,1)S(1)} collective-permute-done((bf16[512,512]{1,0:T(8,128)(2,1)S(1)}, bf16[512,512]{1,0:T(8,128)(2,1)S(1)}, u32[]{:S(2)}, u32[]{:S(2)}) %collective-permute-start.10) | collective-permute-done | bytes 524320 | tf_op jit(solution)/shard_map/ppermute | solution.py:41
  546.7 58.6 %while.28 = (s32[]{:T(128)}, bf16[6,512,128]{1,2,0:T(8,128)(2,1)S(1)}, s32[6]{0:T(128)S(1)}, bf16[512,6,128]{0,2,1:T(8,128)(2,1)S(1)}, bf16[2560,2,128]{2,0,1:T(...) while((s32[]{:T(128)}, ...), condition=%wide.region_10.13_spmd.clone, body=%wide.region_7.12_spmd.clone.sunk | while | flops 686947328 | bytes 17853756 | solution.py:89
  551.2 3.4 fusion.87
  561.0 3.4 fusion.87
  570.7 3.4 fusion.87
  580.5 3.4 fusion.87
  590.3 3.4 fusion.87
  600.0 3.4 fusion.87
  (138 shorter events, 77.8 us)
Async XLA Ops:
  8.0 12.3 %copy-start = (s32[8]{0:T(128)S(1)}, s32[8]{0:T(128)}, u32[]{:S(2)}) copy-start(s32[8]{0:T(128)} %param.26) | copy-start | bytes 100
  8.0 14.4 %copy-start.4 = (s32[8]{0:T(128)S(1)}, s32[8]{0:T(128)}, u32[]{:S(2)}) copy-start(s32[8]{0:T(128)} %param.27) | copy-start | bytes 100
  8.0 332.9 %reduce-scatter.2.cloned.1.call-start = ((), (), s32[]{:S(2)}) async-start(), calls=%async_computation.1 | async-start | bytes 7864320 | tf_op jit(solution)/shard_map/reduce_scatter | solution.py:117
  11.0 38.2 %collective-permute-start = (bf16[512,1536]{0,1:T(8,128)(2,1)S(1)}, bf16[512,1536]{0,1:T(8,128)(2,1)}, u32[]{:S(2)}, u32[]{:S(2)}) collective-permute-start(bf16[512,1536]{0,1:T(8,128)(2,1)S(1)} %pad_maximum_fusion.2), channel_id=1, source_target_pairs={{0,16},{4,20},{8,24},{12,28},{1,17},{5,21},{9,25},{13,29},{2,18},{... | collective-permute-start | bytes 4718600 | tf_op jit(solution)/shard_map/ppermute | solution.py:41
  12.3 71.6 %collective-permute-start.1 = (bf16[512,1536]{0,1:T(8,128)(2,1)S(1)}, bf16[512,1536]{0,1:T(8,128)(2,1)}, u32[]{:S(2)}, u32[]{:S(2)}) collective-permute-start(bf16[512,1536]{0,1:T(8,128)(2,1)S(1)} %pad_maximum_fusion.2), channel_id=1, source_target_pairs={{0,12},{4,16},{8,20},{12,24},{16,28},{1,13},{5,17},{9,21},{13,25},... | collective-permute-start | bytes 4718600 | tf_op jit(solution)/shard_map/ppermute | solution.py:41
  16.5 134.9 %collective-permute-start.2 = (bf16[512,1536]{0,1:T(8,128)(2,1)S(1)}, bf16[512,1536]{0,1:T(8,128)(2,1)}, u32[]{:S(2)}, u32[]{:S(2)}) collective-permute-start(bf16[512,1536]{0,1:T(8,128)(2,1)S(1)} %pad_maximum_fusion.2), channel_id=1, source_target_pairs={{0,8},{4,12},{8,16},{12,20},{16,24},{20,28},{1,9},{5,13},{9,17},{1... | collective-permute-start | bytes 4718600 | tf_op jit(solution)/shard_map/ppermute | solution.py:41
  18.4 201.3 %collective-permute-start.3 = (bf16[512,1536]{0,1:T(8,128)(2,1)S(1)}, bf16[512,1536]{0,1:T(8,128)(2,1)}, u32[]{:S(2)}, u32[]{:S(2)}) collective-permute-start(bf16[512,1536]{0,1:T(8,128)(2,1)S(1)} %pad_maximum_fusion.2), channel_id=1, source_target_pairs={{0,4},{4,8},{8,12},{12,16},{16,20},{20,24},{24,28},{1,5},{5,9},{9,... | collective-permute-start | bytes 4718600 | tf_op jit(solution)/shard_map/ppermute | solution.py:41
  284.1 1.1 copy-start.3
  284.2 182.0 %all-gather.5.cloned.1.call-start = ((), (), s32[]{:S(2)}) async-start(), calls=%async_computation.3 | async-start | bytes 3538944 | tf_op jit(solution)/shard_map/all_gather | solution.py:130
  284.7 181.4 %all-gather.3.cloned.1.call-start = ((), (), s32[]{:S(2)}) async-start(), calls=%async_computation.2 | async-start | bytes 3932160 | tf_op jit(solution)/shard_map/all_gather | solution.py:126
  285.2 17.3 %collective-permute-start.4 = (bf16[1,384,768]{2,1,0:T(8,128)(2,1)S(1)}, bf16[1,384,768]{2,1,0:T(8,128)(2,1)S(1)}, u32[]{:S(2)}, u32[]{:S(2)}) collective-permute-start(bf16[1,384,768]{2,1,0:T(8,128)(2,1)S(1)} %bitcast.107), channel_id=1, source_target_pairs={{0,4},{4,0},{8,12},{12,8},{16,20},{20,16},{24,28},{28,24},{1,5},{5... | collective-permute-start | bytes 1769480 | tf_op jit(solution)/shard_map/ppermute | solution.py:27
  302.9 56.5 %collective-permute-start.5 = (bf16[2,384,768]{2,1,0:T(8,128)(2,1)S(1)}, bf16[2,384,768]{2,1,0:T(8,128)(2,1)}, u32[]{:S(2)}, u32[]{:S(2)}) collective-permute-start(bf16[2,384,768]{2,1,0:T(8,128)(2,1)S(1)} %get-tuple-element.311), channel_id=1, source_target_pairs={{0,8},{4,12},{8,0},{12,4},{16,24},{20,28},{24,16},{28,20},{1,9},{5... | collective-permute-start | bytes 3538952 | tf_op jit(solution)/shard_map/ppermute | solution.py:27
  342.9 18.1 %copy-start.2 = (bf16[512,768]{1,0:T(8,128)(2,1)}, bf16[512,768]{1,0:T(8,128)(2,1)S(1)}, u32[]{:S(2)}) copy-start(bf16[512,768]{1,0:T(8,128)(2,1)S(1)} %get-tuple-element.301) | copy-start | bytes 2359300
  361.4 99.6 %collective-permute-start.6 = (bf16[4,384,768]{2,1,0:T(8,128)(2,1)S(1)}, bf16[4,384,768]{2,1,0:T(8,128)(2,1)}, u32[]{:S(2)}, u32[]{:S(2)}) collective-permute-start(bf16[4,384,768]{2,1,0:T(8,128)(2,1)S(1)} %bitcast.98), channel_id=1, source_target_pairs={{0,16},{4,20},{8,24},{12,28},{16,0},{20,4},{24,8},{28,12},{1,17},{... | collective-permute-start | bytes 7077896 | tf_op jit(solution)/shard_map/ppermute | solution.py:27
  466.1 18.4 %copy-start.1 = (bf16[2,4,384,768]{3,2,1,0:T(8,128)(2,1)S(1)}, bf16[2,4,384,768]{3,2,1,0:T(8,128)(2,1)}, u32[]{:S(2)}) copy-start(bf16[2,4,384,768]{3,2,1,0:T(8,128)(2,1)} %reverse_select_fusion) | copy-start | bytes 14155780
  466.1 18.4 %copy-start.5 = (bf16[512,3072]{1,0:T(8,128)(2,1)S(1)}, bf16[512,3072]{1,0:T(8,128)(2,1)}, u32[]{:S(2)}) copy-start(bf16[512,3072]{1,0:T(8,128)(2,1)} %all-gather.3.cloned.1.call-done) | copy-start | bytes 9437188
  470.9 16.5 %collective-permute-start.7 = (bf16[512,512]{1,0:T(8,128)(2,1)S(1)}, bf16[512,512]{1,0:T(8,128)(2,1)}, u32[]{:S(2)}, u32[]{:S(2)}) collective-permute-start(bf16[512,512]{1,0:T(8,128)(2,1)S(1)} %convolution_convert_fusion.1), channel_id=1, source_target_pairs={{0,16},{4,20},{8,24},{12,28},{1,17},{5,21},{9,25},{13,29},{2,18},{... | collective-permute-start | bytes 1572872 | tf_op jit(solution)/shard_map/ppermute | solution.py:41
  472.2 30.5 %collective-permute-start.8 = (bf16[512,512]{1,0:T(8,128)(2,1)S(1)}, bf16[512,512]{1,0:T(8,128)(2,1)}, u32[]{:S(2)}, u32[]{:S(2)}) collective-permute-start(bf16[512,512]{1,0:T(8,128)(2,1)S(1)} %convolution_convert_fusion.1), channel_id=1, source_target_pairs={{0,12},{4,16},{8,20},{12,24},{16,28},{1,13},{5,17},{9,21},{13,25},... | collective-permute-start | bytes 1572872 | tf_op jit(solution)/shard_map/ppermute | solution.py:41
  480.7 40.9 %collective-permute-start.9 = (bf16[512,512]{1,0:T(8,128)(2,1)S(1)}, bf16[512,512]{1,0:T(8,128)(2,1)S(1)}, u32[]{:S(2)}, u32[]{:S(2)}) collective-permute-start(bf16[512,512]{1,0:T(8,128)(2,1)S(1)} %convolution_convert_fusion.1), channel_id=1, source_target_pairs={{0,8},{4,12},{8,16},{12,20},{16,24},{20,28},{1,9},{5,13},{9,17},{1... | collective-permute-start | bytes 1572872 | tf_op jit(solution)/shard_map/ppermute | solution.py:41
  482.6 62.3 %collective-permute-start.10 = (bf16[512,512]{1,0:T(8,128)(2,1)S(1)}, bf16[512,512]{1,0:T(8,128)(2,1)S(1)}, u32[]{:S(2)}, u32[]{:S(2)}) collective-permute-start(bf16[512,512]{1,0:T(8,128)(2,1)S(1)} %convolution_convert_fusion.1), channel_id=1, source_target_pairs={{0,4},{4,8},{8,12},{12,16},{16,20},{20,24},{24,28},{1,5},{5,9},{9,... | collective-permute-start | bytes 1572872 | tf_op jit(solution)/shard_map/ppermute | solution.py:41
Sparse Core Ops, SparseCore 0:
  284.3 56.6 reduce-scatter.1
Sparse Core Ops, SparseCore 1:
  286.8 73.4 all-gather.4
  362.3 28.6 all-gather.2
